TPU v7x, 128 devices: a whole 4x4x4 slice. The times are simulated.
128 devices in a mesh: img: 1, cfg: 64 (over z, y, x), patch: 2 (over core).
Axes of the slice: x: 4, y: 4, z: 4, core: 2. Of those that a mesh axis runs over, the one named last changes fastest.
Arguments:
- latent: bfloat16 [32, 512, 384], P('img', 'patch')
- cond_vec: float32 [64, 2, 384], P(('img', 'cfg'))
- sched_coef: float32 [3, 2], replicated
- w_ada: bfloat16 [12, 384, 2304], replicated
- w_qkv: bfloat16 [12, 384, 1152], replicated
- w_out: bfloat16 [12, 6, 64, 384], replicated
- w_up: bfloat16 [12, 384, 1536], replicated
- w_down: bfloat16 [12, 1536, 384], replicated
- w_head: bfloat16 [384, 384], replicated
- k_stale: bfloat16 [64, 12, 512, 384], P(('img', 'cfg'))
- v_stale: bfloat16 [64, 12, 512, 384], P(('img', 'cfg'))
Outputs:
- output 1: float32 [64, 512, 384], P(('img', 'cfg'), 'patch')
- output 2: bfloat16 [64, 12, 512, 384], P(('img', 'cfg'))
- output 3: bfloat16 [64, 12, 512, 384], P(('img', 'cfg'))
All inputs are finite; a program needn't handle non-finite values.
Results may differ from a plain program's by a relative error of at most 0.0175248.
Values are sent between devices in bfloat16 or wider.
A program may use at most 1 GiB of HBM per device.

v0:
```python
import jax
import jax.numpy as jnp
from jax import lax
from jax.sharding import PartitionSpec as P


def layer_norm(values):
    row_mean = jnp.mean(values, -1, keepdims=True)
    centered = values - row_mean
    row_var = jnp.mean(centered * centered, -1, keepdims=True)
    return centered * lax.rsqrt(row_var + 1e-6)


def attend(queries, key_set, value_set, n_heads, head_dim):
    local_rows = queries.shape[0]
    tokens = key_set.shape[0]
    q_blk = min(local_rows, 128)
    blocks = queries.reshape(local_rows // q_blk, q_blk, n_heads, head_dim)
    key_h = key_set.reshape(tokens, n_heads, head_dim)
    val_h = value_set.reshape(tokens, n_heads, head_dim)
    score_scale = head_dim ** -0.5

    def one_block(q_part):
        scores = jnp.einsum("qhe,khe->hqk", q_part, key_h, preferred_element_type=jnp.float32) * score_scale
        row_max = jnp.max(scores, -1, keepdims=True)
        weights = jnp.exp(scores - row_max)
        row_sum = jnp.sum(weights, -1)
        mixed_out = jnp.einsum("hqk,khe->qhe", weights.astype(jnp.bfloat16), val_h, preferred_element_type=jnp.float32)
        return (mixed_out / row_sum.T[:, :, None]).astype(jnp.bfloat16)

    return lax.map(one_block, blocks).reshape(local_rows, n_heads, head_dim)


def solution(mesh):
    n_cfg = mesh.shape["cfg"]
    partner = [(dev_pos, dev_pos ^ 1) for dev_pos in range(n_cfg)]
    slot_spec = P(("img", "cfg"), None, None)
    cache_spec = P(("img", "cfg"), None, None, None)
    rep_spec = P()

    def local_step(latent, cond_vec, sched_coef, w_ada, w_qkv, w_out, w_up, w_down, w_head, k_stale, v_stale):
        n_layers = k_stale.shape[1]
        local_rows = latent.shape[1]
        n_heads = w_out.shape[1]
        head_dim = w_out.shape[2]
        cfg_slot = lax.axis_index("cfg")
        row_start = lax.axis_index("patch") * local_rows
        is_cond = cfg_slot % 2 == 0
        latent_now = lax.dynamic_index_in_dim(latent, cfg_slot // 2, axis=0, keepdims=False).astype(jnp.float32)
        mod_all = jnp.einsum("td,lde->tle", jax.nn.silu(cond_vec[0]).astype(jnp.bfloat16), w_ada, preferred_element_type=jnp.float32)
        k_cache = [k_stale[0, layer_idx] for layer_idx in range(n_layers)]
        v_cache = [v_stale[0, layer_idx] for layer_idx in range(n_layers)]
        for step_idx in range(sched_coef.shape[1]):
            resid_now = latent_now
            k_next = []
            v_next = []
            for layer_idx in range(n_layers):
                shift_attn, scale_attn, gate_attn, shift_mlp, scale_mlp, gate_mlp = jnp.split(mod_all[step_idx, layer_idx], 6)
                norm_attn = (layer_norm(resid_now) * (1.0 + scale_attn) + shift_attn).astype(jnp.bfloat16)
                qkv_all = jnp.dot(norm_attn, w_qkv[layer_idx], preferred_element_type=jnp.float32).astype(jnp.bfloat16)
                q_new, k_new, v_new = jnp.split(qkv_all, 3, axis=-1)
                k_next.append(lax.all_gather(k_new, "patch", axis=0, tiled=True))
                v_next.append(lax.all_gather(v_new, "patch", axis=0, tiled=True))
                key_set = lax.dynamic_update_slice(k_cache[layer_idx], k_new, (row_start, 0))
                value_set = lax.dynamic_update_slice(v_cache[layer_idx], v_new, (row_start, 0))
                heads_out = attend(q_new, key_set, value_set, n_heads, head_dim)
                attn_out = jnp.einsum("qhe,hed->qd", heads_out, w_out[layer_idx], preferred_element_type=jnp.float32)
                resid_now = resid_now + gate_attn * attn_out
                norm_mlp = (layer_norm(resid_now) * (1.0 + scale_mlp) + shift_mlp).astype(jnp.bfloat16)
                mlp_up = jnp.dot(norm_mlp, w_up[layer_idx], preferred_element_type=jnp.float32)
                mlp_act = jax.nn.gelu(mlp_up, approximate=True).astype(jnp.bfloat16)
                mlp_down = jnp.dot(mlp_act, w_down[layer_idx], preferred_element_type=jnp.float32)
                resid_now = resid_now + gate_mlp * mlp_down
            k_cache = k_next
            v_cache = v_next
            eps_own = jnp.dot(layer_norm(resid_now).astype(jnp.bfloat16), w_head, preferred_element_type=jnp.float32).astype(jnp.bfloat16)
            eps_peer = lax.ppermute(eps_own, "cfg", partner)
            eps_cond = jnp.where(is_cond, eps_own, eps_peer).astype(jnp.float32)
            eps_unc = jnp.where(is_cond, eps_peer, eps_own).astype(jnp.float32)
            guided = eps_unc + sched_coef[2, step_idx] * (eps_cond - eps_unc)
            latent_now = sched_coef[0, step_idx] * latent_now + sched_coef[1, step_idx] * guided
        return latent_now[None], jnp.stack(k_cache)[None], jnp.stack(v_cache)[None]

    return jax.shard_map(
        local_step,
        mesh=mesh,
        in_specs=(P("img", "patch", None), slot_spec, rep_spec, rep_spec, rep_spec, rep_spec, rep_spec, rep_spec, rep_spec, cache_spec, cache_spec),
        out_specs=(P(("img", "cfg"), "patch", None), cache_spec, cache_spec),
        check_vma=False,
    )
```

profile of v0, /device:TPU:1, one launch (start us, length us, event | category | flops | bytes accessed | tf_op | source)
XLA Modules:
  0.0 512.6 jit_solution(6505414009193251699)
XLA Ops:
  0.7 9.9 %fusion.1370 = f32[2,12,2304]{2,0,1:T(2,128)S(1)} fusion(bf16[12,384,2304]{2,1,0:T(8,128)(2,1)} %param.62, f32[1,2,384]{2,1,0:T(2,128)} %param.60), kind=kOutput, calls=%fused_computation.1646 | convolution fusion | flops 42471168 | bytes 21457920 | tf_op jit(solution)/shard_map/td,lde->tle/dot_general | solution.py:50
  16.8 4.1 slice_bitcast_fusion.1
  20.9 4.1 slice_bitcast_fusion
  35.5 3.6 while.240
  42.1 3.4 fusion.1522
  53.1 4.5 while.241
  60.0 3.0 fusion.1526
  70.0 4.5 while.242
  76.9 3.0 fusion.1530
  86.9 4.7 while.243
  94.0 3.0 fusion.1534
  104.0 4.5 while.244
  110.9 3.0 fusion.1538
  120.9 4.7 while.245
  128.1 3.0 fusion.1542
  138.0 4.5 while.246
  144.9 3.0 fusion.1546
  154.8 4.5 while.247
  161.7 3.0 fusion.1550
  171.6 5.0 while.248
  179.0 3.0 fusion.1554
  186.2 3.2 while.249
  191.5 3.0 fusion.1558
  198.0 3.1 while.250
  202.7 2.8 fusion.1562
  209.0 3.3 while.251
  213.9 2.8 fusion.1566
  223.1 2.5 all_gather.144
  225.6 2.2 all_gather.145
  227.8 2.2 all_gather.146
  232.2 2.2 all_gather.148
  276.4 3.1 fusion.1470
  285.3 4.5 while.252
  291.5 2.8 fusion.1570
  299.2 4.5 while.253
  305.6 2.8 fusion.1574
  313.9 4.7 while.254
  320.5 2.8 fusion.1578
  328.8 4.5 while.255
  335.2 2.8 fusion.1582
  343.5 4.5 while.256
  349.9 2.8 fusion.1586
  358.1 4.9 while.257
  364.9 2.8 fusion.1590
  373.1 4.5 while.258
  379.5 2.8 fusion.1594
  387.8 4.7 while.259
  394.3 2.8 fusion.1598
  402.6 4.5 while.260
  409.0 2.8 fusion.1602
  417.3 4.5 while.261
  423.6 2.8 fusion.1606
  431.8 4.7 while.262
  438.3 2.8 fusion.1610
  445.9 3.2 while.263
  450.8 2.9 fusion.1614
  454.4 2.4 all_gather.168
  456.9 2.2 all_gather.169
  459.1 2.2 all_gather.170
  461.3 2.2 all_gather.171
  463.5 2.2 all_gather.172
  465.8 2.2 all_gather.173
  483.4 2.2 all_gather.181
  509.7 2.7 fusion.920
  (1197 shorter events, 385.4 us)
Async XLA Ops:
  0.6 216.4 %copy-start = (bf16[384,384]{1,0:T(8,128)(2,1)S(1)}, bf16[384,384]{1,0:T(8,128)(2,1)}, u32[]{:S(2)}) copy-start(bf16[384,384]{1,0:T(8,128)(2,1)} %param.67) | copy-start | bytes 884740
  10.6 5.6 %copy-start.24 = (f32[2,12,2304]{2,0,1:T(2,128)}, f32[2,12,2304]{2,0,1:T(2,128)S(1)}, u32[]{:S(2)}) copy-start(f32[2,12,2304]{2,0,1:T(2,128)S(1)} %fusion.1370) | copy-start | bytes 663556
  27.8 4.6 copy-start.4
  53.1 4.5 copy-start.244
  70.0 4.5 copy-start.238
  86.9 4.7 copy-start.230
  104.0 4.5 copy-start.218
  120.9 4.7 copy-start.204
  213.9 8.5 %copy-start.164 = (f32[3,2]{0,1:T(2,128)S(1)}, f32[3,2]{0,1:T(2,128)}, u32[]{:S(2)}) copy-start(f32[3,2]{0,1:T(2,128)} %param.61) | copy-start | bytes 76
  216.8 6.3 %copy-start.26 = (bf16[256,384]{1,0:T(8,128)(2,1)S(1)}, bf16[256,384]{1,0:T(8,128)(2,1)}, u32[]{:S(2)}) copy-start(bf16[256,384]{1,0:T(8,128)(2,1)} %get-tuple-element.1491) | copy-start | bytes 589828
  216.8 8.8 %copy-start.25 = (bf16[256,384]{1,0:T(8,128)(2,1)S(1)}, bf16[256,384]{1,0:T(8,128)(2,1)}, u32[]{:S(2)}) copy-start(bf16[256,384]{1,0:T(8,128)(2,1)} %get-tuple-element.1488) | copy-start | bytes 589828
  216.8 11.0 %copy-start.29 = (bf16[256,384]{1,0:T(8,128)(2,1)S(1)}, bf16[256,384]{1,0:T(8,128)(2,1)}, u32[]{:S(2)}) copy-start(bf16[256,384]{1,0:T(8,128)(2,1)} %get-tuple-element.1486) | copy-start | bytes 589828
  217.0 15.2 %copy-start.32 = (bf16[256,384]{1,0:T(8,128)(2,1)S(1)}, bf16[256,384]{1,0:T(8,128)(2,1)}, u32[]{:S(2)}) copy-start(bf16[256,384]{1,0:T(8,128)(2,1)} %get-tuple-element.1481) | copy-start | bytes 589828
  217.4 17.1 %copy-start.31 = (bf16[256,384]{1,0:T(8,128)(2,1)S(1)}, bf16[256,384]{1,0:T(8,128)(2,1)}, u32[]{:S(2)}) copy-start(bf16[256,384]{1,0:T(8,128)(2,1)} %get-tuple-element.1478) | copy-start | bytes 589828
  217.4 59.1 %collective-permute-start = (bf16[256,384]{1,0:T(8,128)(2,1)S(1)}, bf16[256,384]{1,0:T(8,128)(2,1)}, u32[]{:S(2)}, u32[]{:S(2)}) collective-permute-start(bf16[256,384]{1,0:T(8,128)(2,1)S(1)} %convolution_convert_fusion.25), channel_id=1, source_target_pairs={{0,2},{2,0},{4,6},{6,4},{8,10},{10,8},{12,14},{14,12},{16,18},{18,... | collective-permute-start | bytes 589832 | tf_op jit(solution)/shard_map/ppermute | solution.py:77
  225.6 11.0 %copy-start.36 = (bf16[256,384]{1,0:T(8,128)(2,1)S(1)}, bf16[256,384]{1,0:T(8,128)(2,1)}, u32[]{:S(2)}) copy-start(bf16[256,384]{1,0:T(8,128)(2,1)} %get-tuple-element.1476) | copy-start | bytes 589828
  227.8 11.0 %copy-start.35 = (bf16[256,384]{1,0:T(8,128)(2,1)S(1)}, bf16[256,384]{1,0:T(8,128)(2,1)}, u32[]{:S(2)}) copy-start(bf16[256,384]{1,0:T(8,128)(2,1)} %get-tuple-element.1473) | copy-start | bytes 589828
  230.0 10.9 %copy-start.40 = (bf16[256,384]{1,0:T(8,128)(2,1)S(1)}, bf16[256,384]{1,0:T(8,128)(2,1)}, u32[]{:S(2)}) copy-start(bf16[256,384]{1,0:T(8,128)(2,1)} %get-tuple-element.1471) | copy-start | bytes 589828
  232.2 10.9 %copy-start.39 = (bf16[256,384]{1,0:T(8,128)(2,1)S(1)}, bf16[256,384]{1,0:T(8,128)(2,1)}, u32[]{:S(2)}) copy-start(bf16[256,384]{1,0:T(8,128)(2,1)} %get-tuple-element.1468) | copy-start | bytes 589828
  234.4 10.8 %copy-start.44 = (bf16[256,384]{1,0:T(8,128)(2,1)S(1)}, bf16[256,384]{1,0:T(8,128)(2,1)}, u32[]{:S(2)}) copy-start(bf16[256,384]{1,0:T(8,128)(2,1)} %get-tuple-element.1466) | copy-start | bytes 589828
  236.6 10.8 %copy-start.43 = (bf16[256,384]{1,0:T(8,128)(2,1)S(1)}, bf16[256,384]{1,0:T(8,128)(2,1)}, u32[]{:S(2)}) copy-start(bf16[256,384]{1,0:T(8,128)(2,1)} %get-tuple-element.1463) | copy-start | bytes 589828
  238.8 10.8 %copy-start.48 = (bf16[256,384]{1,0:T(8,128)(2,1)S(1)}, bf16[256,384]{1,0:T(8,128)(2,1)}, u32[]{:S(2)}) copy-start(bf16[256,384]{1,0:T(8,128)(2,1)} %get-tuple-element.1461) | copy-start | bytes 589828
  240.9 10.8 %copy-start.47 = (bf16[256,384]{1,0:T(8,128)(2,1)S(1)}, bf16[256,384]{1,0:T(8,128)(2,1)}, u32[]{:S(2)}) copy-start(bf16[256,384]{1,0:T(8,128)(2,1)} %get-tuple-element.1458) | copy-start | bytes 589828
  243.1 10.8 %copy-start.52 = (bf16[256,384]{1,0:T(8,128)(2,1)S(1)}, bf16[256,384]{1,0:T(8,128)(2,1)}, u32[]{:S(2)}) copy-start(bf16[256,384]{1,0:T(8,128)(2,1)} %get-tuple-element.1456) | copy-start | bytes 589828
  245.2 10.8 %copy-start.51 = (bf16[256,384]{1,0:T(8,128)(2,1)S(1)}, bf16[256,384]{1,0:T(8,128)(2,1)}, u32[]{:S(2)}) copy-start(bf16[256,384]{1,0:T(8,128)(2,1)} %get-tuple-element.1453) | copy-start | bytes 589828
  247.4 10.8 %copy-start.56 = (bf16[256,384]{1,0:T(8,128)(2,1)S(1)}, bf16[256,384]{1,0:T(8,128)(2,1)}, u32[]{:S(2)}) copy-start(bf16[256,384]{1,0:T(8,128)(2,1)} %get-tuple-element.1451) | copy-start | bytes 589828
  249.6 10.8 %copy-start.55 = (bf16[256,384]{1,0:T(8,128)(2,1)S(1)}, bf16[256,384]{1,0:T(8,128)(2,1)}, u32[]{:S(2)}) copy-start(bf16[256,384]{1,0:T(8,128)(2,1)} %get-tuple-element.1448) | copy-start | bytes 589828
  251.7 10.8 %copy-start.60 = (bf16[256,384]{1,0:T(8,128)(2,1)S(1)}, bf16[256,384]{1,0:T(8,128)(2,1)}, u32[]{:S(2)}) copy-start(bf16[256,384]{1,0:T(8,128)(2,1)} %get-tuple-element.1446) | copy-start | bytes 589828
  253.9 10.8 %copy-start.59 = (bf16[256,384]{1,0:T(8,128)(2,1)S(1)}, bf16[256,384]{1,0:T(8,128)(2,1)}, u32[]{:S(2)}) copy-start(bf16[256,384]{1,0:T(8,128)(2,1)} %get-tuple-element.1443) | copy-start | bytes 589828
  256.1 10.7 %copy-start.64 = (bf16[256,384]{1,0:T(8,128)(2,1)S(1)}, bf16[256,384]{1,0:T(8,128)(2,1)}, u32[]{:S(2)}) copy-start(bf16[256,384]{1,0:T(8,128)(2,1)} %get-tuple-element.1441) | copy-start | bytes 589828
  258.2 10.5 %copy-start.63 = (bf16[256,384]{1,0:T(8,128)(2,1)S(1)}, bf16[256,384]{1,0:T(8,128)(2,1)}, u32[]{:S(2)}) copy-start(bf16[256,384]{1,0:T(8,128)(2,1)} %get-tuple-element.1438) | copy-start | bytes 589828
  260.4 10.4 %copy-start.68 = (bf16[256,384]{1,0:T(8,128)(2,1)S(1)}, bf16[256,384]{1,0:T(8,128)(2,1)}, u32[]{:S(2)}) copy-start(bf16[256,384]{1,0:T(8,128)(2,1)} %get-tuple-element.1436) | copy-start | bytes 589828
  262.5 10.3 %copy-start.66 = (bf16[256,384]{1,0:T(8,128)(2,1)S(1)}, bf16[256,384]{1,0:T(8,128)(2,1)}, u32[]{:S(2)}) copy-start(bf16[256,384]{1,0:T(8,128)(2,1)} %get-tuple-element.1433) | copy-start | bytes 589828
  268.8 11.0 %copy-start.181 = (f32[384]{0:T(512)S(1)}, f32[384]{0:T(512)}, u32[]{:S(2)}) copy-start(f32[384]{0:T(512)} %get-tuple-element.984) | copy-start | bytes 4612
  268.8 11.0 %copy-start.182 = (f32[384]{0:T(512)S(1)}, f32[384]{0:T(512)}, u32[]{:S(2)}) copy-start(f32[384]{0:T(512)} %get-tuple-element.985) | copy-start | bytes 4612
  279.6 10.2 %copy-start.1 = (f32[256,384]{1,0:T(8,128)}, f32[256,384]{1,0:T(8,128)S(1)}, u32[]{:S(2)}) copy-start(f32[256,384]{1,0:T(8,128)S(1)} %get-tuple-element.1300) | copy-start | bytes 1179652
  299.2 4.5 copy-start.174
  313.9 4.7 copy-start.168
  328.8 4.6 copy-start.229
  343.5 4.5 copy-start.217
  453.6 5.5 %copy-start.34 = (bf16[256,384]{1,0:T(8,128)(2,1)S(1)}, bf16[256,384]{1,0:T(8,128)(2,1)}, u32[]{:S(2)}) copy-start(bf16[256,384]{1,0:T(8,128)(2,1)} %get-tuple-element.1421) | copy-start | bytes 589828
  453.9 7.5 %copy-start.38 = (bf16[256,384]{1,0:T(8,128)(2,1)S(1)}, bf16[256,384]{1,0:T(8,128)(2,1)}, u32[]{:S(2)}) copy-start(bf16[256,384]{1,0:T(8,128)(2,1)} %get-tuple-element.1416) | copy-start | bytes 589828
  454.2 54.5 %collective-permute-start.1 = (bf16[256,384]{1,0:T(8,128)(2,1)S(1)}, bf16[256,384]{1,0:T(8,128)(2,1)S(1)}, u32[]{:S(2)}, u32[]{:S(2)}) collective-permute-start(bf16[256,384]{1,0:T(8,128)(2,1)S(1)} %convolution_convert_fusion.24), channel_id=1, source_target_pairs={{0,2},{2,0},{4,6},{6,4},{8,10},{10,8},{12,14},{14,12},{16,18},{18,... | collective-permute-start | bytes 589832 | tf_op jit(solution)/shard_map/ppermute | solution.py:77
  454.4 9.1 %copy-start.42 = (bf16[256,384]{1,0:T(8,128)(2,1)S(1)}, bf16[256,384]{1,0:T(8,128)(2,1)}, u32[]{:S(2)}) copy-start(bf16[256,384]{1,0:T(8,128)(2,1)} %get-tuple-element.1411) | copy-start | bytes 589828
  456.8 8.9 %copy-start.46 = (bf16[256,384]{1,0:T(8,128)(2,1)S(1)}, bf16[256,384]{1,0:T(8,128)(2,1)}, u32[]{:S(2)}) copy-start(bf16[256,384]{1,0:T(8,128)(2,1)} %get-tuple-element.1406) | copy-start | bytes 589828
  456.9 11.1 %copy-start.50 = (bf16[256,384]{1,0:T(8,128)(2,1)S(1)}, bf16[256,384]{1,0:T(8,128)(2,1)}, u32[]{:S(2)}) copy-start(bf16[256,384]{1,0:T(8,128)(2,1)} %get-tuple-element.1401) | copy-start | bytes 589828
  459.1 11.1 %copy-start.54 = (bf16[256,384]{1,0:T(8,128)(2,1)S(1)}, bf16[256,384]{1,0:T(8,128)(2,1)}, u32[]{:S(2)}) copy-start(bf16[256,384]{1,0:T(8,128)(2,1)} %get-tuple-element.1396) | copy-start | bytes 589828
  461.3 11.1 %copy-start.58 = (bf16[256,384]{1,0:T(8,128)(2,1)S(1)}, bf16[256,384]{1,0:T(8,128)(2,1)}, u32[]{:S(2)}) copy-start(bf16[256,384]{1,0:T(8,128)(2,1)} %get-tuple-element.1391) | copy-start | bytes 589828
  463.5 10.9 %copy-start.62 = (bf16[256,384]{1,0:T(8,128)(2,1)S(1)}, bf16[256,384]{1,0:T(8,128)(2,1)}, u32[]{:S(2)}) copy-start(bf16[256,384]{1,0:T(8,128)(2,1)} %get-tuple-element.1386) | copy-start | bytes 589828
  465.7 10.9 %copy-start.67 = (bf16[256,384]{1,0:T(8,128)(2,1)S(1)}, bf16[256,384]{1,0:T(8,128)(2,1)}, u32[]{:S(2)}) copy-start(bf16[256,384]{1,0:T(8,128)(2,1)} %get-tuple-element.1381) | copy-start | bytes 589828
  468.0 10.9 %copy-start.70 = (bf16[256,384]{1,0:T(8,128)(2,1)S(1)}, bf16[256,384]{1,0:T(8,128)(2,1)}, u32[]{:S(2)}) copy-start(bf16[256,384]{1,0:T(8,128)(2,1)} %get-tuple-element.1376) | copy-start | bytes 589828
  470.2 10.9 %copy-start.27 = (bf16[256,384]{1,0:T(8,128)(2,1)S(1)}, bf16[256,384]{1,0:T(8,128)(2,1)}, u32[]{:S(2)}) copy-start(bf16[256,384]{1,0:T(8,128)(2,1)} %get-tuple-element.1428) | copy-start | bytes 589828
  474.5 8.9 %copy-start.30 = (bf16[256,384]{1,0:T(8,128)(2,1)S(1)}, bf16[256,384]{1,0:T(8,128)(2,1)}, u32[]{:S(2)}) copy-start(bf16[256,384]{1,0:T(8,128)(2,1)} %get-tuple-element.1423) | copy-start | bytes 589828
  476.7 8.9 %copy-start.33 = (bf16[256,384]{1,0:T(8,128)(2,1)S(1)}, bf16[256,384]{1,0:T(8,128)(2,1)}, u32[]{:S(2)}) copy-start(bf16[256,384]{1,0:T(8,128)(2,1)} %get-tuple-element.1418) | copy-start | bytes 589828
  478.9 8.9 %copy-start.37 = (bf16[256,384]{1,0:T(8,128)(2,1)S(1)}, bf16[256,384]{1,0:T(8,128)(2,1)}, u32[]{:S(2)}) copy-start(bf16[256,384]{1,0:T(8,128)(2,1)} %get-tuple-element.1413) | copy-start | bytes 589828
  481.1 8.9 %copy-start.41 = (bf16[256,384]{1,0:T(8,128)(2,1)S(1)}, bf16[256,384]{1,0:T(8,128)(2,1)}, u32[]{:S(2)}) copy-start(bf16[256,384]{1,0:T(8,128)(2,1)} %get-tuple-element.1408) | copy-start | bytes 589828
  483.3 8.9 %copy-start.45 = (bf16[256,384]{1,0:T(8,128)(2,1)S(1)}, bf16[256,384]{1,0:T(8,128)(2,1)}, u32[]{:S(2)}) copy-start(bf16[256,384]{1,0:T(8,128)(2,1)} %get-tuple-element.1403) | copy-start | bytes 589828
  483.4 11.1 %copy-start.49 = (bf16[256,384]{1,0:T(8,128)(2,1)S(1)}, bf16[256,384]{1,0:T(8,128)(2,1)}, u32[]{:S(2)}) copy-start(bf16[256,384]{1,0:T(8,128)(2,1)} %get-tuple-element.1398) | copy-start | bytes 589828
  485.6 11.1 %copy-start.53 = (bf16[256,384]{1,0:T(8,128)(2,1)S(1)}, bf16[256,384]{1,0:T(8,128)(2,1)}, u32[]{:S(2)}) copy-start(bf16[256,384]{1,0:T(8,128)(2,1)} %get-tuple-element.1393) | copy-start | bytes 589828
  487.8 10.9 %copy-start.57 = (bf16[256,384]{1,0:T(8,128)(2,1)S(1)}, bf16[256,384]{1,0:T(8,128)(2,1)}, u32[]{:S(2)}) copy-start(bf16[256,384]{1,0:T(8,128)(2,1)} %get-tuple-element.1388) | copy-start | bytes 589828
  490.0 10.8 %copy-start.61 = (bf16[256,384]{1,0:T(8,128)(2,1)S(1)}, bf16[256,384]{1,0:T(8,128)(2,1)}, u32[]{:S(2)}) copy-start(bf16[256,384]{1,0:T(8,128)(2,1)} %get-tuple-element.1383) | copy-start | bytes 589828
  492.2 10.7 %copy-start.65 = (bf16[256,384]{1,0:T(8,128)(2,1)S(1)}, bf16[256,384]{1,0:T(8,128)(2,1)}, u32[]{:S(2)}) copy-start(bf16[256,384]{1,0:T(8,128)(2,1)} %get-tuple-element.1378) | copy-start | bytes 589828
  494.5 10.5 %copy-start.69 = (bf16[256,384]{1,0:T(8,128)(2,1)S(1)}, bf16[256,384]{1,0:T(8,128)(2,1)}, u32[]{:S(2)}) copy-start(bf16[256,384]{1,0:T(8,128)(2,1)} %get-tuple-element.1373) | copy-start | bytes 589828
  507.9 4.5 copy-start.163
  (243 other events, 388.0 us)
where the time goes:
time: 521 us; the launch traced here: 513 us
  matrix products  208 us (40%)
  local copies, waits for them, and re-layouts  138 us (26%)
  blocking collectives  104 us (20%)
  other arithmetic  51.5 us (10%)
    dot_general x24, matrix products, local_step(): jnp.dot(mlp_act, w_down[layer_idx], preferred_element_type=jnp.float32)  70.4 us
    all_gather x24, blocking collectives, local_step(): k_next.append(lax.all_gather(k_new, 'patch', axis=0, tiled=True))  52.7 us
    all_gather x24, blocking collectives, local_step(): v_next.append(lax.all_gather(v_new, 'patch', axis=0, tiled=True))  51.5 us
    dot_general x24, matrix products, local_step(): jnp.dot(norm_attn, w_qkv[layer_idx], preferred_element_type=jnp.float32)  41.2 us
    dot_general x24, matrix products, local_step(): jnp.einsum('qhe,hed->qd', heads_out, w_out[layer_idx], preferred_element_...  37.2 us
    dynamic_update_slice x24, local copies, waits for them, and re-layouts, local_step(): lax.dynamic_update_slice(v_cache[layer_idx], v_new, (row_start, 0))  30.1 us
    while x236, local copies, waits for them, and re-layouts  26.8 us
    split x48, local copies, waits for them, and re-layouts, local_step(): q_new, k_new, v_new = jnp.split(qkv_all, 3, axis=-1)  26.4 us
  transfers between devices with their start and end apart: 2, of which 0 were waited for; matrix products, arithmetic and copies ran while one was open for 1% of the time, Pallas kernels for 0%

commit v1 on v0

v1 whole, which is shorter than its diff:
```python
import functools
import math

import jax
import jax.numpy as jnp
from jax import lax
from jax.experimental import pallas as pl
from jax.experimental.pallas import tpu as pltpu
from jax.sharding import PartitionSpec as P

MESH = pl.DeviceIdType.MESH
F32 = jnp.float32
BF16 = jnp.bfloat16
GELU_A = math.sqrt(2.0 / math.pi)
GELU_B = GELU_A * 0.044715


def normed(values):
    row_mean = jnp.mean(values, -1, keepdims=True)
    centered = values - row_mean
    row_var = jnp.mean(centered * centered, -1, keepdims=True)
    return centered * lax.rsqrt(row_var + 1e-6)


def gelu(x):
    half = 0.5 * x
    return half + half * jnp.tanh(x * (GELU_A + GELU_B * (x * x)))


def contract(a, b, a_dim, b_dim):
    return lax.dot_general(a, b, (((a_dim,), (b_dim,)), ((), ())), preferred_element_type=F32)


def kernel(
    n_steps, n_layers, n_heads, head_dim,
    latent_hbm, cond_ref, sched_ref, ada_ref, qkv_ref, out_ref, up_ref, down_ref, head_ref, k_stale, v_stale,
    x_out, k_out, v_out,
    lat_buf, resid, mod_buf, o_buf, kv_own, kv_peer, eps_send, eps_recv,
    lat_sem, stale_sem, send_sem, recv_sem, last_sem, keep_sem, eps_send_sem, eps_recv_sem,
):
    step = pl.program_id(0)
    layer = pl.program_id(1)
    rows, width = resid.shape
    patch = lax.axis_index("patch")
    slot = lax.axis_index("cfg")
    other = 1 - patch
    partner = slot + 1 - 2 * (slot % 2)
    my_rows = pl.ds(pl.multiple_of(patch * rows, rows), rows)
    peer_rows = pl.ds(pl.multiple_of(other * rows, rows), rows)
    own = (step * n_layers + layer) % 2
    last_step = n_steps - 1
    first = (step == 0) & (layer == 0)

    def load_stale(at_layer):
        place = n_layers + at_layer % 2
        return [
            pltpu.make_async_copy(src.at[0, at_layer, peer_rows], kv_peer.at[place, part], stale_sem.at[at_layer % 2, part])
            for part, src in enumerate((k_stale, v_stale))
        ]

    def send_fresh(at_layer, at_slot):
        return [
            pltpu.make_async_remote_copy(
                src_ref=kv_own.at[at_slot, part], dst_ref=kv_peer.at[at_layer, part],
                send_sem=send_sem.at[at_slot, part], recv_sem=recv_sem.at[at_layer, part],
                device_id={"patch": other}, device_id_type=MESH)
            for part in range(2)
        ]

    def send_final(at_layer, at_slot):
        return [
            pltpu.make_async_remote_copy(
                src_ref=kv_own.at[at_slot, part], dst_ref=dst.at[0, at_layer, my_rows],
                send_sem=send_sem.at[at_slot, part], recv_sem=last_sem.at[at_layer, part],
                device_id={"patch": other}, device_id_type=MESH)
            for part, dst in enumerate((k_out, v_out))
        ]

    def keep_final(at_layer, at_slot):
        return [
            pltpu.make_async_copy(kv_own.at[at_slot, part], dst.at[0, at_layer, my_rows], keep_sem.at[at_slot, part])
            for part, dst in enumerate((k_out, v_out))
        ]

    def send_eps():
        return pltpu.make_async_remote_copy(
            src_ref=eps_send, dst_ref=eps_recv.at[step],
            send_sem=eps_send_sem, recv_sem=eps_recv_sem.at[step],
            device_id={"cfg": partner}, device_id_type=MESH)

    @pl.when(first)
    def _():
        barrier = pltpu.get_barrier_semaphore()
        pl.semaphore_signal(barrier, inc=1, device_id={"patch": other}, device_id_type=MESH)
        pl.semaphore_signal(barrier, inc=1, device_id={"cfg": partner}, device_id_type=MESH)
        fetch = pltpu.make_async_copy(latent_hbm.at[slot // 2], lat_buf, lat_sem)
        fetch.start()
        for copy in load_stale(0):
            copy.start()
        fetch.wait()
        x_out[0] = lat_buf[...].astype(F32)
        pl.semaphore_wait(barrier, 2)

    @pl.when(step == 0)
    def _():
        cond = cond_ref[0]
        act = (cond * jax.nn.sigmoid(cond)).astype(BF16)
        mod_buf[layer, 0:n_steps, :] = jnp.dot(act, ada_ref[0], preferred_element_type=F32)

        for copy in load_stale(layer):
            copy.wait()

        @pl.when(layer + 1 < n_layers)
        def _():
            for copy in load_stale(layer + 1):
                copy.start()

    @pl.when(step > 0)
    def _():
        for copy in send_fresh(layer, own):
            copy.wait_recv()

    @pl.when(layer == 0)
    def _():
        resid[...] = x_out[0]

    def mod(part):
        return mod_buf[layer, pl.ds(step, 1), part * width:(part + 1) * width]

    h = (normed(resid[...]) * (1.0 + mod(1)) + mod(0)).astype(BF16)
    qkv = jnp.dot(h, qkv_ref[0], preferred_element_type=F32).astype(BF16)

    @pl.when((step > 0) | (layer >= 2))
    def _():
        for copy in send_fresh(layer, own):
            copy.wait_send()

    @pl.when((step == last_step) & (layer >= 2))
    def _():
        for copy in keep_final(layer, own):
            copy.wait()

    kv_own[own, 0] = qkv[:, width:2 * width]
    kv_own[own, 1] = qkv[:, 2 * width:]

    place = jnp.where(step == 0, n_layers + layer % 2, layer)
    factor = head_dim ** -0.5 * math.log2(math.e)
    pair_width = 2 * head_dim
    lane = lax.broadcasted_iota(jnp.int32, (rows, pair_width), 1)
    for pair in range(n_heads // 2):
        cols = slice(pair * pair_width, (pair + 1) * pair_width)
        q_pair = qkv[:, cols]
        k_mine = kv_own[own, 0, :, cols]
        k_peer = kv_peer[place, 0, :, cols]
        v_mine = kv_own[own, 1, :, cols].T
        v_peer = kv_peer[place, 1, :, cols].T
        for sub in range(2):
            keep = (lane < head_dim) if sub == 0 else (lane >= head_dim)
            q_head = jnp.where(keep, q_pair, jnp.zeros_like(q_pair))
            s_mine = contract(k_mine, q_head, 1, 1)
            s_peer = contract(k_peer, q_head, 1, 1)
            top = jnp.maximum(jnp.max(s_mine, 0, keepdims=True), jnp.max(s_peer, 0, keepdims=True))
            e_mine = jnp.exp2((s_mine - top) * factor)
            e_peer = jnp.exp2((s_peer - top) * factor)
            total = jnp.sum(e_mine, 0, keepdims=True) + jnp.sum(e_peer, 0, keepdims=True)
            part = slice(sub * head_dim, (sub + 1) * head_dim)
            mixed = contract(v_mine[part], e_mine.astype(BF16), 1, 0) + contract(v_peer[part], e_peer.astype(BF16), 1, 0)
            base = (2 * pair + sub) * head_dim
            o_buf[base:base + head_dim, :] = (mixed * (1.0 / total)).astype(BF16)

    attn = contract(o_buf[...], out_ref[0], 0, 0)
    r = resid[...] + mod(2) * attn

    @pl.when(step < last_step)
    def _():
        for copy in send_fresh(layer, own):
            copy.start()

    @pl.when(step == last_step)
    def _():
        for copy in send_final(layer, own) + keep_final(layer, own):
            copy.start()

    h2 = (normed(r) * (1.0 + mod(4)) + mod(3)).astype(BF16)
    chunk = 512
    down = None
    for base in range(0, up_ref.shape[2], chunk):
        up = jnp.dot(h2, up_ref[0, :, base:base + chunk], preferred_element_type=F32)
        act = gelu(up).astype(BF16)
        term = jnp.dot(act, down_ref[0, base:base + chunk, :], preferred_element_type=F32)
        down = term if down is None else down + term
    r = r + mod(5) * down
    resid[...] = r

    @pl.when(layer == n_layers - 1)
    def _():
        eps = jnp.dot(normed(resid[...]).astype(BF16), head_ref[...], preferred_element_type=F32)

        @pl.when(step > 0)
        def _():
            send_eps().wait_send()

        eps_send[...] = eps.astype(BF16)
        send_eps().start()
        send_eps().wait_recv()
        mine = eps_send[...].astype(F32)
        peer = eps_recv[step].astype(F32)
        is_cond = slot % 2 == 0
        eps_cond = jnp.where(is_cond, mine, peer)
        eps_unc = jnp.where(is_cond, peer, mine)
        guided = eps_unc + sched_ref[2, step] * (eps_cond - eps_unc)
        x_out[0] = sched_ref[0, step] * x_out[0] + sched_ref[1, step] * guided

    @pl.when((step == last_step) & (layer == n_layers - 1))
    def _():
        send_eps().wait_send()
        for at_layer in (n_layers - 2, n_layers - 1):
            at_slot = (last_step * n_layers + at_layer) % 2
            for copy in send_final(at_layer, at_slot):
                copy.wait_send()
            for copy in keep_final(at_layer, at_slot):
                copy.wait()
        for at_layer in range(n_layers):
            for copy in send_final(at_layer, at_layer % 2):
                copy.wait_recv()


def solution(mesh):
    slot_spec = P(("img", "cfg"), None, None)
    cache_spec = P(("img", "cfg"), None, None, None)
    rep_spec = P()

    def local_step(latent, cond_vec, sched_coef, w_ada, w_qkv, w_out, w_up, w_down, w_head, k_stale, v_stale):
        n_layers, width = w_qkv.shape[0], w_qkv.shape[1]
        rows = latent.shape[1]
        n_heads, head_dim = w_out.shape[1], w_out.shape[2]
        n_steps = sched_coef.shape[1]
        w_out = w_out.reshape(n_layers, width, width)

        def per_layer(array):
            return pl.BlockSpec((1,) + array.shape[1:], lambda s, l: (l, 0, 0))

        any_spec = pl.BlockSpec(memory_space=pl.ANY)
        vmem_spec = pl.BlockSpec(memory_space=pltpu.VMEM)
        x_new, k_new, v_new = pl.pallas_call(
            functools.partial(kernel, n_steps, n_layers, n_heads, head_dim),
            grid=(n_steps, n_layers),
            out_shape=[
                jax.ShapeDtypeStruct((1, rows, width), F32),
                jax.ShapeDtypeStruct(k_stale.shape, BF16),
                jax.ShapeDtypeStruct(v_stale.shape, BF16),
            ],
            in_specs=[
                any_spec,
                vmem_spec,
                pl.BlockSpec(memory_space=pltpu.SMEM),
                pl.BlockSpec((1,) + w_ada.shape[1:], lambda s, l: (jnp.where(s == 0, l, n_layers - 1), 0, 0)),
                per_layer(w_qkv),
                per_layer(w_out),
                per_layer(w_up),
                per_layer(w_down),
                vmem_spec,
                any_spec,
                any_spec,
            ],
            out_specs=[vmem_spec, any_spec, any_spec],
            scratch_shapes=[
                pltpu.VMEM((rows, width), BF16),
                pltpu.VMEM((rows, width), F32),
                pltpu.VMEM((n_layers, 8, 6 * width), F32),
                pltpu.VMEM((width, rows), BF16),
                pltpu.VMEM((2, 2, rows, width), BF16),
                pltpu.VMEM((n_layers + 2, 2, rows, width), BF16),
                pltpu.VMEM((rows, width), BF16),
                pltpu.VMEM((n_steps, rows, width), BF16),
                pltpu.SemaphoreType.DMA,
                pltpu.SemaphoreType.DMA((2, 2)),
                pltpu.SemaphoreType.DMA((2, 2)),
                pltpu.SemaphoreType.DMA((n_layers, 2)),
                pltpu.SemaphoreType.DMA((n_layers, 2)),
                pltpu.SemaphoreType.DMA((2, 2)),
                pltpu.SemaphoreType.DMA,
                pltpu.SemaphoreType.DMA((n_steps,)),
            ],
            compiler_params=pltpu.CompilerParams(
                collective_id=0, has_side_effects=True, vmem_limit_bytes=48 * 1024 * 1024,
                dimension_semantics=("arbitrary", "arbitrary"),
            ),
            name="denoise",
        )(latent, cond_vec, sched_coef, w_ada, w_qkv, w_out, w_up, w_down, w_head, k_stale, v_stale)
        return x_new, k_new, v_new

    return jax.shard_map(
        local_step,
        mesh=mesh,
        in_specs=(P("img", "patch", None), slot_spec, rep_spec, rep_spec, rep_spec, rep_spec, rep_spec, rep_spec, rep_spec, cache_spec, cache_spec),
        out_specs=(P(("img", "cfg"), "patch", None), cache_spec, cache_spec),
        check_vma=False,
    )
```

time: 521 us -> 153 us (0.29); the launches traced: 513 us -> 151 us
  matrix products: 208 us -> 0 us
  Pallas kernels: 0 us -> 138 us
  local copies, waits for them, and re-layouts: 138 us -> 12.9 us
  blocking collectives: 104 us -> 0 us
  other arithmetic: 51.5 us -> 0.01 us
    dot_general x171 -> x0, matrix products: 208 us -> none  [the longest x24 70.4 us: local_step(): jnp.dot(mlp_act, w_down[layer_idx], preferred_element_type=jnp.float32)]
    pallas_call x0 -> x1, Pallas kernels: none -> 138 us  [local_step(): pl.pallas_call(functools.partial(kernel, n_steps, n_layers, n_heads, head...]
    all_gather x48 -> x0, blocking collectives: 104 us -> none  [the longest x24 52.7 us: local_step(): k_next.append(lax.all_gather(k_new, 'patch', axis=0, tiled=True))]
    dynamic_update_slice x48 -> x0, local copies, waits for them, and re-layouts: 43.4 us -> none  [the longest x24 30.1 us: local_step(): lax.dynamic_update_slice(v_cache[layer_idx], v_new, (row_start, 0))]
    reduce_sum x100 -> x0, other arithmetic: 38.6 us -> none  [the longest x48 24.1 us: one_block(): row_sum = jnp.sum(weights, -1)]
    while x260 -> x0, local copies, waits for them, and re-layouts: 28.4 us -> none
    split x48 -> x0, local copies, waits for them, and re-layouts: 26.4 us -> none  [local_step(): q_new, k_new, v_new = jnp.split(qkv_all, 3, axis=-1)]
    another operation x26 -> x0, local copies, waits for them, and re-layouts: 13.8 us -> none
  transfers between devices with their start and end apart: 2 -> 0, of which waited for: 0 -> 0; matrix products, arithmetic and copies ran while one was open for 1% -> 0% of each run, Pallas kernels for 0% -> 0%
where the time goes in v1:
time: 153 us; the launch traced here: 151 us
  Pallas kernels  138 us (90%)
  local copies, waits for them, and re-layouts  12.9 us (8%)
    pallas_call x1, Pallas kernels, local_step(): pl.pallas_call(functools.partial(kernel, n_steps, n_layers, n_heads, head...  138 us
    unnamed x14, local copies, waits for them, and re-layouts  12.9 us

profile of v1, /device:TPU:1, one launch (start us, length us, event | category | flops | bytes accessed | tf_op | source)
XLA Modules:
  0.0 151.2 jit_solution(5031130228067174829)
XLA Ops:
  0.6 0.8 copy.14.sched_ref
  1.4 0.0 copy-start
  1.4 2.0 %copy-done = bf16[12,6,64,384]{3,2,1,0:T(8,128)(2,1)S(1)} copy-done((bf16[12,6,64,384]{3,2,1,0:T(8,128)(2,1)S(1)}, bf16[12,6,64,384]{3,2,1,0:T(8,128)(2,1)}, u32[]{:S(2)}) %copy-start) | copy-done | bytes 3538968
  3.4 0.0 copy-start.1
  3.4 1.0 copy-done.1
  4.4 0.0 copy-start.2
  4.4 0.7 copy-done.2
  5.0 137.7 %denoise.1 = (f32[1,256,384]{2,1,0:T(8,128)S(1)}, bf16[1,12,512,384]{3,2,1,0:T(8,128)(2,1)}, bf16[1,12,512,384]{3,2,1,0:T(8,128)(2,1)}) custom-call(bf16[32,256,384]{2,1,0:T(8,128)(2,1)} %latent_hbm.1, f32[1,2,384]{2,1,0:T(2,128)S(1)} %copy-done.2, f32[3,2]{1,0:T(4,128)S(1)} %copy.14.sched_ref, bf16[12,384,2304]{2,1,0:T(8,128)(2,1)} %ada_ref.1, ...), custom_call_target="tpu_custom_call" | custom-call | tf_op jit(solution)/shard_map/denoise/pallas_call | solution.py:245
  142.8 0.0 slice-start
  142.8 0.7 copy.18
  143.5 0.0 slice-start.1
  143.5 5.5 %copy.19 = bf16[1,12,512,384]{3,2,1,0:T(8,128)(2,1)} copy(bf16[1,12,512,384]{3,2,1,0:T(8,128)(2,1)} %get-tuple-element.7) | data formatting | bytes 9437184
  149.0 0.0 slice-done
  149.0 0.0 slice-done.1
  149.0 2.2 %copy.20 = bf16[1,12,512,384]{3,2,1,0:T(8,128)(2,1)} copy(bf16[1,12,512,384]{3,2,1,0:T(8,128)(2,1)S(1)} %bitcast.3) | data formatting | bytes 9437184
  (1 shorter events, 0.0 us)
Async XLA Ops:
  1.4 2.0 %copy-start = (bf16[12,6,64,384]{3,2,1,0:T(8,128)(2,1)S(1)}, bf16[12,6,64,384]{3,2,1,0:T(8,128)(2,1)}, u32[]{:S(2)}) copy-start(bf16[12,6,64,384]{3,2,1,0:T(8,128)(2,1)} %param.16) | copy-start | bytes 10616836
  3.4 1.0 copy-start.1
  4.4 0.7 copy-start.2
  142.8 6.3 %slice-start = ((s8[4718592]{0:T(1024)(128)(4,1)}), s8[4194304]{0:T(1024)(128)(4,1)S(1)}, s32[]{:S(2)}) async-start(s8[4718592]{0:T(1024)(128)(4,1)} %bitcast.2), calls=%async_computation | async-start | bytes 8388608
  143.5 5.5 %slice-start.1 = ((s8[4718592]{0:T(1024)(128)(4,1)}), s8[524288]{0:T(1024)(128)(4,1)S(1)}, s32[]{:S(2)}) async-start(s8[4718592]{0:T(1024)(128)(4,1)} %bitcast.2), calls=%async_computation.1 | async-start | bytes 1048576

commit v2 on v1

v2 whole, which is shorter than its diff:
```python
import functools
import math

import jax
import jax.numpy as jnp
from jax import lax
from jax.experimental import pallas as pl
from jax.experimental.pallas import tpu as pltpu
from jax.sharding import PartitionSpec as P

MESH = pl.DeviceIdType.MESH
F32 = jnp.float32
BF16 = jnp.bfloat16
VMEM_ALL = 67043328
GELU_A = math.sqrt(2.0 / math.pi)
GELU_B = GELU_A * 0.044715


def normed(values):
    row_mean = jnp.mean(values, -1, keepdims=True)
    centered = values - row_mean
    row_var = jnp.mean(centered * centered, -1, keepdims=True)
    return centered * lax.rsqrt(row_var + 1e-6)


def gelu(x):
    half = 0.5 * x
    return half + half * jnp.tanh(x * (GELU_A + GELU_B * (x * x)))


def contract(a, b, a_dim, b_dim):
    return lax.dot_general(a, b, (((a_dim,), (b_dim,)), ((), ())), preferred_element_type=F32)


def kernel(
    n_steps, n_layers, n_heads, head_dim,
    latent_hbm, cond_ref, sched_ref, ada_ref, qkv_ref, out_ref, up_ref, down_ref, head_ref, k_stale, v_stale,
    x_out, eps_out, kv_fin,
    lat_buf, resid, mod_buf, o_buf, s_buf, p_buf, kv_own, kv_peer, eps_recv,
    lat_sem, stale_sem, send_sem, recv_sem, last_sem, keep_sem, eps_send_sem, eps_recv_sem,
):
    step = pl.program_id(0)
    layer = pl.program_id(1)
    rows, width = resid.shape
    patch = lax.axis_index("patch")
    slot = lax.axis_index("cfg")
    other = 1 - patch
    partner = slot + 1 - 2 * (slot % 2)
    peer_rows = pl.ds(pl.multiple_of(other * rows, rows), rows)
    last_step = n_steps - 1
    first = (step == 0) & (layer == 0)

    def load_stale(at_layer):
        place = n_layers + at_layer % 2
        return [
            pltpu.make_async_copy(src.at[0, at_layer, peer_rows], kv_peer.at[place, part], stale_sem.at[at_layer % 2, part])
            for part, src in enumerate((k_stale, v_stale))
        ]

    def send_kv(at_layer, target, arrival):
        return [
            pltpu.make_async_remote_copy(
                src_ref=kv_own.at[at_layer, part], dst_ref=target.at[at_layer, part],
                send_sem=send_sem.at[at_layer, part], recv_sem=arrival.at[at_layer, part],
                device_id={"patch": other}, device_id_type=MESH)
            for part in range(2)
        ]

    def send_fresh(at_layer):
        return send_kv(at_layer, kv_peer, recv_sem)

    def send_final(at_layer):
        return send_kv(at_layer, kv_fin.at[1], last_sem)

    def keep_final(at_layer):
        return [
            pltpu.make_async_copy(kv_own.at[at_layer, part], kv_fin.at[0, at_layer, part], keep_sem.at[at_layer, part])
            for part in range(2)
        ]

    def send_eps():
        return pltpu.make_async_remote_copy(
            src_ref=eps_out, dst_ref=eps_recv.at[step],
            send_sem=eps_send_sem, recv_sem=eps_recv_sem.at[step],
            device_id={"cfg": partner}, device_id_type=MESH)

    @pl.when(first)
    def _():
        barrier = pltpu.get_barrier_semaphore()
        pl.semaphore_signal(barrier, inc=1, device_id={"patch": other}, device_id_type=MESH)
        pl.semaphore_signal(barrier, inc=1, device_id={"cfg": partner}, device_id_type=MESH)
        fetch = pltpu.make_async_copy(latent_hbm.at[slot // 2], lat_buf, lat_sem)
        fetch.start()
        for copy in load_stale(0):
            copy.start()
        fetch.wait()
        x_out[...] = lat_buf[...].astype(F32)
        pl.semaphore_wait(barrier, 2)

    @pl.when(step == 0)
    def _():
        cond = cond_ref[0]
        act = (cond * jax.nn.sigmoid(cond)).astype(BF16)
        mod_buf[layer, 0:n_steps, :] = jnp.dot(act, ada_ref[0], preferred_element_type=F32)

        for copy in load_stale(layer):
            copy.wait()

        @pl.when(layer + 1 < n_layers)
        def _():
            for copy in load_stale(layer + 1):
                copy.start()

    @pl.when(step > 0)
    def _():
        for copy in send_fresh(layer):
            copy.wait_recv()
            copy.wait_send()

    @pl.when(layer == 0)
    def _():
        resid[...] = x_out[...]

    def mod(part):
        return mod_buf[layer, pl.ds(step, 1), part * width:(part + 1) * width]

    h = (normed(resid[...]) * (1.0 + mod(1)) + mod(0)).astype(BF16)
    qkv = jnp.dot(h, qkv_ref[0], preferred_element_type=F32).astype(BF16)

    kv_own[layer, 0] = qkv[:, width:2 * width]
    kv_own[layer, 1] = qkv[:, 2 * width:]

    place = jnp.where(step == 0, n_layers + layer % 2, layer)
    factor = head_dim ** -0.5 * math.log2(math.e)
    pair_width = 2 * head_dim
    lane = lax.broadcasted_iota(jnp.int32, (rows, pair_width), 1)
    tops, totals = {}, {}

    def cols_of(head):
        base = head // 2 * pair_width
        return slice(base, base + pair_width)

    def score(head):
        cols = cols_of(head)
        keep = (lane < head_dim) if head % 2 == 0 else (lane >= head_dim)
        q_head = jnp.where(keep, qkv[:, cols], jnp.zeros((rows, pair_width), BF16))
        top = None
        for side, keys in enumerate((kv_own[layer, 0, :, cols], kv_peer[place, 0, :, cols])):
            s = contract(keys, q_head, 1, 1)
            s_buf[head % 2, side] = s
            side_top = jnp.max(s, 0, keepdims=True)
            top = side_top if top is None else jnp.maximum(top, side_top)
        tops[head] = top

    def weigh(head):
        total = None
        for side in range(2):
            e = jnp.exp2((s_buf[head % 2, side] - tops[head]) * factor)
            p_buf[head % 2, side] = e.astype(BF16)
            side_total = jnp.sum(e, 0, keepdims=True)
            total = side_total if total is None else total + side_total
        totals[head] = total

    def mix(head):
        cols = cols_of(head)
        part = slice(head % 2 * head_dim, (head % 2 + 1) * head_dim)
        mixed = None
        for side, values in enumerate((kv_own[layer, 1, :, cols], kv_peer[place, 1, :, cols])):
            term = contract(values.T[part], p_buf[head % 2, side], 1, 0)
            mixed = term if mixed is None else mixed + term
        o_buf[head * head_dim:(head + 1) * head_dim, :] = (mixed * (1.0 / totals[head])).astype(BF16)

    for turn in range(n_heads + 2):
        if turn < n_heads:
            score(turn)
        if 1 <= turn <= n_heads:
            weigh(turn - 1)
        if turn >= 2:
            mix(turn - 2)

    attn = contract(o_buf[...], out_ref[0], 0, 0)
    r = resid[...] + mod(2) * attn

    h2 = (normed(r) * (1.0 + mod(4)) + mod(3)).astype(BF16)
    chunk = 512
    down = None
    for base in range(0, up_ref.shape[2], chunk):
        up = jnp.dot(h2, up_ref[0, :, base:base + chunk], preferred_element_type=F32)
        act = gelu(up).astype(BF16)
        term = jnp.dot(act, down_ref[0, base:base + chunk, :], preferred_element_type=F32)
        down = term if down is None else down + term
    r = r + mod(5) * down
    resid[...] = r

    @pl.when(step < last_step)
    def _():
        for copy in send_fresh(layer):
            copy.start()

    @pl.when(step == last_step)
    def _():
        for copy in send_final(layer) + keep_final(layer):
            copy.start()

    @pl.when(layer == n_layers - 1)
    def _():
        @pl.when((step > 0) & (step < n_steps))
        def _():
            send_eps().wait_send()

        eps = jnp.dot(normed(resid[...]).astype(BF16), head_ref[...], preferred_element_type=F32)
        eps_out[...] = eps.astype(BF16)

    @pl.when((step < last_step) & (layer == n_layers - 1))
    def _():
        send_eps().start()
        send_eps().wait_recv()
        x_out[...] = guide(slot, sched_ref, step, x_out[...], eps_out[...], eps_recv[step])

    @pl.when((step == last_step) & (layer == n_layers - 1))
    def _():
        for at_layer in range(n_layers):
            for copy in send_final(at_layer):
                copy.wait_send()
                copy.wait_recv()
            for copy in keep_final(at_layer):
                copy.wait()


def guide(slot, sched, step, x, mine, peer):
    mine, peer = mine.astype(F32), peer.astype(F32)
    is_cond = slot % 2 == 0
    eps_cond = jnp.where(is_cond, mine, peer)
    eps_unc = jnp.where(is_cond, peer, mine)
    guided = eps_unc + sched[step, 2] * (eps_cond - eps_unc)
    return sched[step, 0] * x + sched[step, 1] * guided


def store_kernel(kv_fin, k_out, v_out, buf, in_sem, out_sem):
    n_layers, rows = buf.shape[1], buf.shape[3]
    patch = lax.axis_index("patch")
    loads, stores = [], []
    for layer in range(n_layers):
        for side, owner in enumerate((patch, 1 - patch)):
            for part, dst in enumerate((k_out, v_out)):
                at = pl.ds(pl.multiple_of(owner * rows, rows), rows)
                here = buf.at[side, layer, part]
                loads.append(pltpu.make_async_copy(kv_fin.at[side, layer, part], here, in_sem.at[side, layer, part]))
                stores.append(pltpu.make_async_copy(here, dst.at[0, layer, at], out_sem.at[side, layer, part]))
    for copy in loads:
        copy.start()
    for load, store in zip(loads, stores):
        load.wait()
        store.start()
    for copy in stores:
        copy.wait()


def solution(mesh):
    slot_spec = P(("img", "cfg"), None, None)
    cache_spec = P(("img", "cfg"), None, None, None)
    rep_spec = P()
    n_cfg = mesh.shape["cfg"]
    partner = [(at, at ^ 1) for at in range(n_cfg)]

    def local_step(latent, cond_vec, sched_coef, w_ada, w_qkv, w_out, w_up, w_down, w_head, k_stale, v_stale):
        n_layers, width = w_qkv.shape[0], w_qkv.shape[1]
        rows = latent.shape[1]
        n_heads, head_dim = w_out.shape[1], w_out.shape[2]
        n_steps = sched_coef.shape[1]
        w_out = w_out.reshape(n_layers, width, width)

        def per_layer(array):
            return pl.BlockSpec((1,) + array.shape[1:], lambda s, l: (l, 0, 0))

        def whole(array):
            return pl.BlockSpec(array.shape, lambda s, l: (0,) * array.ndim)

        any_spec = pl.BlockSpec(memory_space=pl.ANY)
        vmem_spec = pl.BlockSpec(memory_space=pltpu.VMEM)
        kv_shape = (2, n_layers, 2, rows, width)
        x_last, eps, kv_fin = pl.pallas_call(
            functools.partial(kernel, n_steps, n_layers, n_heads, head_dim),
            grid=(n_steps, n_layers),
            out_shape=[
                jax.ShapeDtypeStruct((rows, width), F32),
                jax.ShapeDtypeStruct((rows, width), BF16),
                jax.ShapeDtypeStruct(kv_shape, BF16),
            ],
            in_specs=[
                any_spec,
                whole(cond_vec),
                pl.BlockSpec(memory_space=pltpu.SMEM),
                pl.BlockSpec((1,) + w_ada.shape[1:], lambda s, l: (jnp.where(s == 0, l, n_layers - 1), 0, 0)),
                per_layer(w_qkv),
                per_layer(w_out),
                per_layer(w_up),
                per_layer(w_down),
                whole(w_head),
                any_spec,
                any_spec,
            ],
            out_specs=[vmem_spec, vmem_spec, any_spec],
            scratch_shapes=[
                pltpu.VMEM((rows, width), BF16),
                pltpu.VMEM((rows, width), F32),
                pltpu.VMEM((n_layers, 8, 6 * width), F32),
                pltpu.VMEM((width, rows), BF16),
                pltpu.VMEM((2, 2, rows, rows), F32),
                pltpu.VMEM((2, 2, rows, rows), BF16),
                pltpu.VMEM((n_layers, 2, rows, width), BF16),
                pltpu.VMEM((n_layers + 2, 2, rows, width), BF16),
                pltpu.VMEM((n_steps, rows, width), BF16),
                pltpu.SemaphoreType.DMA,
                pltpu.SemaphoreType.DMA((2, 2)),
                pltpu.SemaphoreType.DMA((n_layers, 2)),
                pltpu.SemaphoreType.DMA((n_layers, 2)),
                pltpu.SemaphoreType.DMA((n_layers, 2)),
                pltpu.SemaphoreType.DMA((n_layers, 2)),
                pltpu.SemaphoreType.DMA,
                pltpu.SemaphoreType.DMA((n_steps,)),
            ],
            compiler_params=pltpu.CompilerParams(
                collective_id=0, has_side_effects=True, vmem_limit_bytes=VMEM_ALL,
                dimension_semantics=("arbitrary", "arbitrary"),
            ),
            name="denoise",
        )(latent, cond_vec, sched_coef.T, w_ada, w_qkv, w_out, w_up, w_down, w_head, k_stale, v_stale)
        eps_peer = lax.ppermute(eps, "cfg", partner)
        k_new, v_new = pl.pallas_call(
            store_kernel,
            out_shape=[jax.ShapeDtypeStruct(k_stale.shape, BF16), jax.ShapeDtypeStruct(v_stale.shape, BF16)],
            in_specs=[any_spec],
            out_specs=[any_spec] * 2,
            scratch_shapes=[
                pltpu.VMEM(kv_shape, BF16),
                pltpu.SemaphoreType.DMA(kv_shape[:3]),
                pltpu.SemaphoreType.DMA(kv_shape[:3]),
            ],
            compiler_params=pltpu.CompilerParams(vmem_limit_bytes=VMEM_ALL),
            cost_estimate=pl.CostEstimate(flops=0, bytes_accessed=2 * 2 * k_stale.size * 2, transcendentals=0),
            name="store",
        )(kv_fin)
        x_new = guide(lax.axis_index("cfg"), sched_coef.T, n_steps - 1, x_last, eps, eps_peer)
        return x_new[None], k_new, v_new

    return jax.shard_map(
        local_step,
        mesh=mesh,
        in_specs=(P("img", "patch", None), slot_spec, rep_spec, rep_spec, rep_spec, rep_spec, rep_spec, rep_spec, rep_spec, cache_spec, cache_spec),
        out_specs=(P(("img", "cfg"), "patch", None), cache_spec, cache_spec),
        check_vma=False,
    )
```

time: 153 us -> 122 us (0.80)
  Pallas kernels: 138 us -> 115 us
  local copies, waits for them, and re-layouts: 12.9 us -> 1.38 us
  other arithmetic: 0.01 us -> 3.86 us
    pallas_call x1, Pallas kernels: 138 us -> 108 us  [local_step(): pl.pallas_call(functools.partial(kernel, n_steps, n_layers, n_heads, head...]
    unnamed x14 -> x0, local copies, waits for them, and re-layouts: 12.9 us -> none
    pallas_call x0 -> x1, Pallas kernels: none -> 7.89 us  [local_step(): pl.pallas_call(store_kernel, out_shape=[jax.ShapeDtypeStruct(k_stale.shap...]
    broadcast_in_dim x0 -> x1, other arithmetic: none -> 3.86 us  [local_step(): return (x_new[None], k_new, v_new)]
  transfers between devices with their start and end apart: 0 -> 1, of which waited for: 0 -> 0; matrix products, arithmetic and copies ran while one was open for 0% -> 1% of each run, Pallas kernels for 0% -> 6%
where the time goes in v2:
time: 122 us
  Pallas kernels  115 us (94%)
  other arithmetic  3.86 us (3%)
  local copies, waits for them, and re-layouts  1.38 us (1%)
    pallas_call x1, Pallas kernels, local_step(): pl.pallas_call(functools.partial(kernel, n_steps, n_layers, n_heads, head...  108 us
    pallas_call x1, Pallas kernels, local_step(): pl.pallas_call(store_kernel, out_shape=[jax.ShapeDtypeStruct(k_stale.shap...  7.89 us
    broadcast_in_dim x1, other arithmetic, local_step(): return (x_new[None], k_new, v_new)  3.86 us
  transfers between devices with their start and end apart: 1, of which 0 were waited for; matrix products, arithmetic and copies ran while one was open for 1% of the time, Pallas kernels for 6%

profile of v2, /device:TPU:1, one launch (start us, length us, event | category | flops | bytes accessed | tf_op | source)
XLA Modules:
  0.0 121.6 jit_solution(8738966867958075343)
XLA Ops:
  0.6 107.5 %denoise.1 = (f32[256,384]{1,0:T(8,128)}, bf16[256,384]{1,0:T(8,128)(2,1)}, bf16[2,12,2,256,384]{4,3,2,1,0:T(8,128)(2,1)}) custom-call(bf16[32,256,384]{2,1,0:T(8,128)(2,1)} %latent_hbm.1, f32[1,2,384]{2,1,0:T(2,128)} %cond_ref.1, f32[2,3]{1,0:T(2,128)} %bitcast.8, bf16[12,384,2304]{2,1,0:T(8,128)(2,1)} %ada_ref.1, bf16[12,384,1152]{2,1,0:T(8,128)(2,1)} %qkv_ref.1, ...), custom_call_target="tpu_custom_call" | custom-call | tf_op jit(solution)/shard_map/denoise/pallas_call | solution.py:282
  108.2 0.2 collective-permute-start
  108.4 7.9 %store.1 = (bf16[1,12,512,384]{3,2,1,0:T(8,128)(2,1)}, bf16[1,12,512,384]{3,2,1,0:T(8,128)(2,1)}) custom-call(bf16[2,12,2,256,384]{4,3,2,1,0:T(8,128)(2,1)} %get-tuple-element.10.kv_fin), custom_call_target="tpu_custom_call" | custom-call | bytes 18874368 | tf_op jit(solution)/shard_map/store/pallas_call | solution.py:330
  116.3 1.4 %fusion.6 = (f32[1,1]{1,0:T(1,128)}, f32[1,1]{1,0:T(1,128)}, f32[1,1]{1,0:T(1,128)}) fusion(f32[2,3]{1,0:T(2,128)} %bitcast.9), kind=kLoop, calls=%fused_computation.8 | loop fusion | bytes 24 | tf_op jit(solution)/shard_map/slice | solution.py:236
  117.7 0.0 collective-permute-done
  117.7 3.9 %fusion.5 = f32[1,256,384]{2,1,0:T(8,128)} fusion(bf16[256,384]{1,0:T(8,128)(2,1)} %get-tuple-element.9, bf16[256,384]{1,0:T(8,128)(2,1)} %collective-permute-done, f32[256,384]{1,0:T(8,128)} %get-tuple-element.8, f32[]{:T(128)} %bitcast.4, f32[]{:T(128)} %bitcast.3, f32[]{:T(128)} %bitcast.1, pred[]{:T(512)S(6)} %eq.5), kind=kLoop, calls=%fused_computation.7 | loop fusion | flops 983040 | bytes 1179661 | tf_op jit(solution)/shard_map/broadcast_in_dim | solution.py:345
Async XLA Ops:
  108.2 9.5 %collective-permute-start = (bf16[256,384]{1,0:T(8,128)(2,1)}, bf16[256,384]{1,0:T(8,128)(2,1)}, u32[]{:S(2)}, u32[]{:S(2)}) collective-permute-start(bf16[256,384]{1,0:T(8,128)(2,1)} %get-tuple-element.9), channel_id=1, source_target_pairs={{0,2},{2,0},{4,6},{6,4},{8,10},{10,8},{12,14},{14,12},{16,18},{18,... | collective-permute-start | bytes 589832 | tf_op jit(solution)/shard_map/ppermute | solution.py:329

commit v3 on v2

v3 whole, which is shorter than its diff:
```python
import functools
import math

import jax
import jax.numpy as jnp
from jax import lax
from jax.experimental import pallas as pl
from jax.experimental.pallas import tpu as pltpu
from jax.sharding import PartitionSpec as P

MESH = pl.DeviceIdType.MESH
F32 = jnp.float32
BF16 = jnp.bfloat16
VMEM_ALL = 67043328
GELU_A = math.sqrt(2.0 / math.pi)
GELU_B = GELU_A * 0.044715


def normed(values):
    row_mean = jnp.mean(values, -1, keepdims=True)
    centered = values - row_mean
    row_var = jnp.mean(centered * centered, -1, keepdims=True)
    return centered * lax.rsqrt(row_var + 1e-6)


def gelu_of_half(half):
    return half + half * jnp.tanh(half * (2.0 * GELU_A + 8.0 * GELU_B * (half * half)))


def contract(a, b, a_dim, b_dim):
    return lax.dot_general(a, b, (((a_dim,), (b_dim,)), ((), ())), preferred_element_type=F32)


def kernel(
    n_steps, n_layers, n_heads, head_dim,
    latent_hbm, cond_hbm, sched_hbm, ada_hbm, qkv_hbm, out_hbm, up_hbm, down_hbm, head_hbm, k_stale, v_stale,
    x_out, eps_out, kv_fin,
    sched_ref, cond_buf, lat_buf, head_buf, ada_buf, qkv_buf, out_buf, up_buf, down_buf,
    resid, mod_buf, o_buf, s_buf, p_buf, kv_own, kv_peer, eps_recv,
    small_sem, ada_sem, weight_sem, stale_sem, send_sem, recv_sem, last_sem, keep_sem, eps_send_sem, eps_recv_sem,
):
    rows, width = resid.shape
    patch = lax.axis_index("patch")
    slot = lax.axis_index("cfg")
    other = 1 - patch
    partner = slot + 1 - 2 * (slot % 2)
    peer_rows = pl.ds(pl.multiple_of(other * rows, rows), rows)
    last_step = n_steps - 1

    def start(copies):
        for copy in copies:
            copy.start()

    def wait(copies):
        for copy in copies:
            copy.wait()

    def load_small():
        pairs = ((latent_hbm.at[slot // 2], lat_buf), (cond_hbm.at[0], cond_buf), (sched_hbm, sched_ref), (head_hbm, head_buf))
        return [pltpu.make_async_copy(src, dst, small_sem.at[at]) for at, (src, dst) in enumerate(pairs)]

    def load_ada(at_layer):
        return [pltpu.make_async_copy(ada_hbm.at[at_layer], ada_buf.at[at_layer % 2], ada_sem.at[at_layer % 2])]

    def load_weights(at_layer):
        pairs = ((qkv_hbm, qkv_buf), (out_hbm, out_buf), (up_hbm, up_buf), (down_hbm, down_buf))
        return [
            pltpu.make_async_copy(src.at[at_layer], dst.at[at_layer % 2], weight_sem.at[at_layer % 2, at])
            for at, (src, dst) in enumerate(pairs)
        ]

    def load_stale(at_layer):
        place = n_layers + at_layer % 2
        return [
            pltpu.make_async_copy(src.at[0, at_layer, peer_rows], kv_peer.at[place, part], stale_sem.at[at_layer % 2, part])
            for part, src in enumerate((k_stale, v_stale))
        ]

    def send_kv(at_layer, target, arrival):
        return [
            pltpu.make_async_remote_copy(
                src_ref=kv_own.at[at_layer, part], dst_ref=target.at[at_layer, part],
                send_sem=send_sem.at[at_layer, part], recv_sem=arrival.at[at_layer, part],
                device_id={"patch": other}, device_id_type=MESH)
            for part in range(2)
        ]

    def send_fresh(at_layer):
        return send_kv(at_layer, kv_peer, recv_sem)

    def send_final(at_layer):
        return send_kv(at_layer, kv_fin.at[1], last_sem)

    def keep_final(at_layer):
        return [
            pltpu.make_async_copy(kv_own.at[at_layer, part], kv_fin.at[0, at_layer, part], keep_sem.at[at_layer, part])
            for part in range(2)
        ]

    def send_eps(at_step):
        return pltpu.make_async_remote_copy(
            src_ref=eps_out, dst_ref=eps_recv.at[at_step],
            send_sem=eps_send_sem, recv_sem=eps_recv_sem.at[at_step],
            device_id={"cfg": partner}, device_id_type=MESH)

    def modulate(at_layer):
        cond = cond_buf[...]
        act = (cond * jax.nn.sigmoid(cond)).astype(BF16)
        mod_buf[at_layer, 0:n_steps, :] = jnp.dot(act, ada_buf[at_layer % 2], preferred_element_type=F32)

    def block(step, layer):
        side = layer % 2
        wait(load_weights(layer))
        if step == 0:
            wait(load_stale(layer))

            @pl.when(layer + 1 < n_layers)
            def _():
                wait(load_ada(layer + 1))
                start(load_stale(layer + 1))

            @pl.when(layer + 2 < n_layers)
            def _():
                start(load_ada(layer + 2))
        else:
            for copy in send_fresh(layer):
                copy.wait_recv()
                copy.wait_send()
        if step < last_step:
            start(load_weights(lax.rem(layer + 1, n_layers)))
        else:
            @pl.when(layer + 1 < n_layers)
            def _():
                start(load_weights(layer + 1))

        def mod(part):
            return mod_buf[layer, step:step + 1, part * width:(part + 1) * width]

        h = (normed(resid[...]) * (1.0 + mod(1)) + mod(0)).astype(BF16)
        qkv = jnp.dot(h, qkv_buf[side], preferred_element_type=F32).astype(BF16)
        kv_own[layer, 0] = qkv[:, width:2 * width]
        kv_own[layer, 1] = qkv[:, 2 * width:]

        place = n_layers + layer % 2 if step == 0 else layer
        factor = head_dim ** -0.5 * math.log2(math.e)
        pair_width = 2 * head_dim
        lane = lax.broadcasted_iota(jnp.int32, (rows, pair_width), 1)
        tops, totals = {}, {}

        def cols_of(head):
            base = head // 2 * pair_width
            return slice(base, base + pair_width)

        def score(head):
            cols = cols_of(head)
            keep = (lane < head_dim) if head % 2 == 0 else (lane >= head_dim)
            q_head = jnp.where(keep, qkv[:, cols], jnp.zeros((rows, pair_width), BF16))
            top = None
            for side, keys in enumerate((kv_own[layer, 0, :, cols], kv_peer[place, 0, :, cols])):
                s = contract(keys, q_head, 1, 1)
                s_buf[head % 2, side] = s
                side_top = jnp.max(s, 0, keepdims=True)
                top = side_top if top is None else jnp.maximum(top, side_top)
            tops[head] = top

        def weigh(head):
            total = None
            for side in range(2):
                e = jnp.exp2((s_buf[head % 2, side] - tops[head]) * factor)
                p_buf[head % 2, side] = e.astype(BF16)
                side_total = jnp.sum(e, 0, keepdims=True)
                total = side_total if total is None else total + side_total
            totals[head] = total

        def mix(head):
            cols = cols_of(head)
            part = slice(head % 2 * head_dim, (head % 2 + 1) * head_dim)
            mixed = None
            for side, values in enumerate((kv_own[layer, 1, :, cols], kv_peer[place, 1, :, cols])):
                term = contract(values.T[part], p_buf[head % 2, side], 1, 0)
                mixed = term if mixed is None else mixed + term
            o_buf[head * head_dim:(head + 1) * head_dim, :] = (mixed * (1.0 / totals[head])).astype(BF16)

        for turn in range(n_heads + 2):
            if turn < n_heads:
                score(turn)
            if 1 <= turn <= n_heads:
                weigh(turn - 1)
            if turn >= 2:
                mix(turn - 2)

        if step == 0:
            modulate(layer + 1)

        attn = contract(o_buf[...], out_buf[side], 0, 0)
        r = resid[...] + mod(2) * attn
        h2 = (normed(r) * (0.5 * (1.0 + mod(4))) + 0.5 * mod(3)).astype(BF16)
        chunk = 512
        down = None
        for base in range(0, up_buf.shape[2], chunk):
            half = jnp.dot(h2, up_buf[side, :, base:base + chunk], preferred_element_type=F32)
            act = gelu_of_half(half).astype(BF16)
            term = jnp.dot(act, down_buf[side, base:base + chunk, :], preferred_element_type=F32)
            down = term if down is None else down + term
        resid[...] = r + mod(5) * down
        if step < last_step:
            start(send_fresh(layer))
        else:
            start(send_final(layer) + keep_final(layer))

    barrier = pltpu.get_barrier_semaphore()
    pl.semaphore_signal(barrier, inc=1, device_id={"patch": other}, device_id_type=MESH)
    pl.semaphore_signal(barrier, inc=1, device_id={"cfg": partner}, device_id_type=MESH)
    start(load_small())
    start(load_ada(0))
    start(load_weights(0))
    start(load_stale(0))
    start(load_ada(1))
    wait(load_small())
    x_out[...] = lat_buf[...].astype(F32)
    resid[...] = lat_buf[...].astype(F32)
    wait(load_ada(0))
    modulate(0)
    pl.semaphore_wait(barrier, 2)

    for step in range(n_steps):
        lax.fori_loop(0, n_layers, lambda layer, carry: (block(step, layer), carry)[1], 0)
        if step > 0:
            send_eps(step - 1).wait_send()
        eps = jnp.dot(normed(resid[...]).astype(BF16), head_buf[...], preferred_element_type=F32)
        eps_out[...] = eps.astype(BF16)
        if step < last_step:
            send_eps(step).start()
            send_eps(step).wait_recv()
            x_now = guide(slot, sched_ref, step, x_out[...], eps_out[...], eps_recv[step])
            x_out[...] = x_now
            resid[...] = x_now

    def drain(at_layer, carry):
        for copy in send_final(at_layer):
            copy.wait_send()
            copy.wait_recv()
        wait(keep_final(at_layer))
        return carry

    lax.fori_loop(0, n_layers, drain, 0)


def guide(slot, sched, step, x, mine, peer):
    mine, peer = mine.astype(F32), peer.astype(F32)
    is_cond = slot % 2 == 0
    eps_cond = jnp.where(is_cond, mine, peer)
    eps_unc = jnp.where(is_cond, peer, mine)
    guided = eps_unc + sched[step, 2] * (eps_cond - eps_unc)
    return sched[step, 0] * x + sched[step, 1] * guided


def store_kernel(kv_fin, k_out, v_out, buf, in_sem, out_sem):
    n_layers, rows = buf.shape[1], buf.shape[3]
    patch = lax.axis_index("patch")
    loads, stores = [], []
    for layer in range(n_layers):
        for side, owner in enumerate((patch, 1 - patch)):
            for part, dst in enumerate((k_out, v_out)):
                at = pl.ds(pl.multiple_of(owner * rows, rows), rows)
                here = buf.at[side, layer, part]
                loads.append(pltpu.make_async_copy(kv_fin.at[side, layer, part], here, in_sem.at[side, layer, part]))
                stores.append(pltpu.make_async_copy(here, dst.at[0, layer, at], out_sem.at[side, layer, part]))
    for copy in loads:
        copy.start()
    for load, store in zip(loads, stores):
        load.wait()
        store.start()
    for copy in stores:
        copy.wait()


def guide_kernel(step, sched_ref, x_ref, mine_ref, peer_ref, x_new):
    x_new[0] = guide(lax.axis_index("cfg"), sched_ref, step, x_ref[...], mine_ref[...], peer_ref[...])


def solution(mesh):
    slot_spec = P(("img", "cfg"), None, None)
    cache_spec = P(("img", "cfg"), None, None, None)
    rep_spec = P()
    n_cfg = mesh.shape["cfg"]
    partner = [(at, at ^ 1) for at in range(n_cfg)]

    def local_step(latent, cond_vec, sched_coef, w_ada, w_qkv, w_out, w_up, w_down, w_head, k_stale, v_stale):
        n_layers, width = w_qkv.shape[0], w_qkv.shape[1]
        rows = latent.shape[1]
        n_heads, head_dim = w_out.shape[1], w_out.shape[2]
        n_steps = sched_coef.shape[1]
        w_out = w_out.reshape(n_layers, width, width)

        any_spec = pl.BlockSpec(memory_space=pl.ANY)
        vmem_spec = pl.BlockSpec(memory_space=pltpu.VMEM)
        kv_shape = (2, n_layers, 2, rows, width)
        x_last, eps, kv_fin = pl.pallas_call(
            functools.partial(kernel, n_steps, n_layers, n_heads, head_dim),
            out_shape=[
                jax.ShapeDtypeStruct((rows, width), F32),
                jax.ShapeDtypeStruct((rows, width), BF16),
                jax.ShapeDtypeStruct(kv_shape, BF16),
            ],
            in_specs=[any_spec] * 11,
            out_specs=[vmem_spec, vmem_spec, any_spec],
            scratch_shapes=[
                pltpu.SMEM(sched_coef.shape[::-1], F32),
                pltpu.VMEM(cond_vec.shape[1:], F32),
                pltpu.VMEM((rows, width), BF16),
                pltpu.VMEM(w_head.shape, BF16),
                pltpu.VMEM((2,) + w_ada.shape[1:], BF16),
                pltpu.VMEM((2,) + w_qkv.shape[1:], BF16),
                pltpu.VMEM((2,) + w_out.shape[1:], BF16),
                pltpu.VMEM((2,) + w_up.shape[1:], BF16),
                pltpu.VMEM((2,) + w_down.shape[1:], BF16),
                pltpu.VMEM((rows, width), F32),
                pltpu.VMEM((n_layers + 1, 8, 6 * width), F32),
                pltpu.VMEM((width, rows), BF16),
                pltpu.VMEM((2, 2, rows, rows), F32),
                pltpu.VMEM((2, 2, rows, rows), BF16),
                pltpu.VMEM((n_layers, 2, rows, width), BF16),
                pltpu.VMEM((n_layers + 2, 2, rows, width), BF16),
                pltpu.VMEM((n_steps, rows, width), BF16),
                pltpu.SemaphoreType.DMA((4,)),
                pltpu.SemaphoreType.DMA((2,)),
                pltpu.SemaphoreType.DMA((2, 4)),
                pltpu.SemaphoreType.DMA((2, 2)),
                pltpu.SemaphoreType.DMA((n_layers, 2)),
                pltpu.SemaphoreType.DMA((n_layers, 2)),
                pltpu.SemaphoreType.DMA((n_layers, 2)),
                pltpu.SemaphoreType.DMA((n_layers, 2)),
                pltpu.SemaphoreType.DMA,
                pltpu.SemaphoreType.DMA((n_steps,)),
            ],
            compiler_params=pltpu.CompilerParams(
                collective_id=0, has_side_effects=True, vmem_limit_bytes=VMEM_ALL,
            ),
            name="denoise",
        )(latent, cond_vec, sched_coef.T, w_ada, w_qkv, w_out, w_up, w_down, w_head, k_stale, v_stale)
        eps_peer = lax.ppermute(eps, "cfg", partner)
        k_new, v_new = pl.pallas_call(
            store_kernel,
            out_shape=[jax.ShapeDtypeStruct(k_stale.shape, BF16), jax.ShapeDtypeStruct(v_stale.shape, BF16)],
            in_specs=[any_spec],
            out_specs=[any_spec] * 2,
            scratch_shapes=[
                pltpu.VMEM(kv_shape, BF16),
                pltpu.SemaphoreType.DMA(kv_shape[:3]),
                pltpu.SemaphoreType.DMA(kv_shape[:3]),
            ],
            compiler_params=pltpu.CompilerParams(vmem_limit_bytes=VMEM_ALL),
            cost_estimate=pl.CostEstimate(flops=0, bytes_accessed=2 * 2 * k_stale.size * 2, transcendentals=0),
            name="store",
        )(kv_fin)
        x_new = pl.pallas_call(
            functools.partial(guide_kernel, n_steps - 1),
            out_shape=jax.ShapeDtypeStruct((1, rows, width), F32),
            in_specs=[pl.BlockSpec(memory_space=pltpu.SMEM)] + [vmem_spec] * 3,
            out_specs=vmem_spec,
            name="guide",
        )(sched_coef.T, x_last, eps, eps_peer)
        return x_new, k_new, v_new

    return jax.shard_map(
        local_step,
        mesh=mesh,
        in_specs=(P("img", "patch", None), slot_spec, rep_spec, rep_spec, rep_spec, rep_spec, rep_spec, rep_spec, rep_spec, cache_spec, cache_spec),
        out_specs=(P(("img", "cfg"), "patch", None), cache_spec, cache_spec),
        check_vma=False,
    )
```

time: 122 us -> 111 us (0.910)
  Pallas kernels: 115 us -> 111 us
  other arithmetic: 3.86 us -> 0 us
  local copies, waits for them, and re-layouts: 1.38 us -> 0 us
    pallas_call x1, Pallas kernels: 108 us -> 101 us  [local_step(): pl.pallas_call(functools.partial(kernel, n_steps, n_layers, n_heads, head...]
    broadcast_in_dim x1 -> x0, other arithmetic: 3.86 us -> none  [local_step(): return (x_new[None], k_new, v_new)]
    pallas_call x0 -> x1, Pallas kernels: none -> 2.06 us  [local_step(): pl.pallas_call(functools.partial(guide_kernel, n_steps - 1), out_shape=ja...]
    slice x1 -> x0, local copies, waits for them, and re-layouts: 1.38 us -> none  [guide(): return sched[step, 0] * x + sched[step, 1] * guided]
  transfers between devices with their start and end apart: 1 -> 1, of which waited for: 0 -> 0; matrix products, arithmetic and copies ran while one was open for 1% -> 0% of each run, Pallas kernels for 6% -> 7%
where the time goes in v3:
time: 111 us
  Pallas kernels  111 us (100%)
    pallas_call x1, Pallas kernels, local_step(): pl.pallas_call(functools.partial(kernel, n_steps, n_layers, n_heads, head...  101 us
    pallas_call x1, Pallas kernels, local_step(): pl.pallas_call(store_kernel, out_shape=[jax.ShapeDtypeStruct(k_stale.shap...  7.9 us
  transfers between devices with their start and end apart: 1, of which 0 were waited for; matrix products, arithmetic and copies ran while one was open for 0% of the time, Pallas kernels for 7%

profile of v3, /device:TPU:1, one launch (start us, length us, event | category | flops | bytes accessed | tf_op | source)
XLA Modules:
  0.0 111.3 jit_solution(291567214359942949)
XLA Ops:
  0.6 100.6 %denoise.1 = (f32[256,384]{1,0:T(8,128)}, bf16[256,384]{1,0:T(8,128)(2,1)}, bf16[2,12,2,256,384]{4,3,2,1,0:T(8,128)(2,1)}) custom-call(bf16[32,256,384]{2,1,0:T(8,128)(2,1)} %latent_hbm.1, f32[1,2,384]{2,1,0:T(2,128)} %cond_hbm.1, f32[2,3]{1,0:T(2,128)} %bitcast.3, bf16[12,384,2304]{2,1,0:T(8,128)(2,1)} %ada_hbm.1, bf16[12,384,1152]{2,1,0:T(8,128)(2,1)} %qkv_hbm.1, ...), custom_call_target="tpu_custom_call" | custom-call | tf_op jit(solution)/shard_map/denoise/pallas_call | solution.py:299
  101.2 0.1 collective-permute-start
  101.3 7.9 %store.1 = (bf16[1,12,512,384]{3,2,1,0:T(8,128)(2,1)}, bf16[1,12,512,384]{3,2,1,0:T(8,128)(2,1)}) custom-call(bf16[2,12,2,256,384]{4,3,2,1,0:T(8,128)(2,1)} %get-tuple-element.10.kv_fin), custom_call_target="tpu_custom_call" | custom-call | bytes 18874368 | tf_op jit(solution)/shard_map/store/pallas_call | solution.py:343
  109.2 0.0 collective-permute-done.peer_ref
  109.2 2.1 %guide.1 = f32[1,256,384]{2,1,0:T(8,128)} custom-call(f32[2,3]{1,0:T(2,128)} %bitcast.4, f32[256,384]{1,0:T(8,128)} %get-tuple-element.8.x_ref, bf16[256,384]{1,0:T(8,128)(2,1)} %get-tuple-element.9.mine_ref, bf16[256,384]{1,0:T(8,128)(2,1)} %collective-permute-done.peer_ref), custom_call_target="tpu_custom_call" | custom-call | tf_op jit(solution)/shard_map/guide/pallas_call | solution.py:357
Async XLA Ops:
  101.2 8.0 %collective-permute-start = (bf16[256,384]{1,0:T(8,128)(2,1)}, bf16[256,384]{1,0:T(8,128)(2,1)}, u32[]{:S(2)}, u32[]{:S(2)}) collective-permute-start(bf16[256,384]{1,0:T(8,128)(2,1)} %get-tuple-element.9.mine_ref), channel_id=1, source_target_pairs={{0,2},{2,0},{4,6},{6,4},{8,10},{10,8},{12,14},{14,12},{16,18},{18,... | collective-permute-start | bytes 589832 | tf_op jit(solution)/shard_map/ppermute | solution.py:342
